TPU v7x, 32 devices: a whole 2x2x4 slice. The times are simulated.
32 devices in a mesh: section: 4 (over x, core), head: 4 (over z), dp: 2 (over y).
Axes of the slice: x: 2, y: 2, z: 4, core: 2. Of those that a mesh axis runs over, the one named last changes fastest.
Arguments:
- teacher_q: bfloat16 [4, 256, 8192], P('section', 'dp', 'head'), may hold values from -150 to 150
- teacher_k: bfloat16 [4, 256, 1024], P('section', 'dp', 'head'), may hold values from -150 to 150
- student_q: bfloat16 [4, 2, 256, 4096], P('section', None, 'dp', 'head'), may hold values from -150 to 150
- student_k: bfloat16 [4, 2, 256, 1024], P('section', None, 'dp', 'head'), may hold values from -150 to 150
- student_scale: float32 [4, 32], P(None, 'head'), may hold values from 0.5 to 2
- pairing: int32 [4], replicated, may hold values from 0 to 3, as said below
- placement: int32 [4], replicated, may hold values from 0 to 3, as said below
Outputs:
- student_q_grad: bfloat16 [4, 2, 256, 4096], P('section', None, 'dp', 'head')
- student_k_grad: bfloat16 [4, 2, 256, 1024], P('section', None, 'dp', 'head')
- layer_kl: float32 [2, 4], P('dp')
- scale_grad: float32 [4, 32], P(None, 'head')
Inputs may be any that keep to these rules, and one draw needn't show every extreme that they name: `pairing`: each teacher layer of the window is paired with exactly one student layer. `placement`: a section holds at most 2 student layers, in increasing order of layer index, and some section holds exactly 2.
All inputs are finite; a program needn't handle non-finite values.
Results may differ from a plain program's by a relative error of at most 0.0048.
Values may be sent and summed in bfloat16 or wider, within the bound.
A program may use at most 64 MiB of HBM per device.

v0:
```python
import math

import jax
import jax.numpy as jnp
from jax import lax
from jax.sharding import PartitionSpec as P

STUDENT_HEADS = 32
HEAD_WIDTH = 128
REPLICA_TOKENS = 128


def causal_mask(length):
    row_ids = lax.broadcasted_iota(jnp.int32, (length, length), 0)
    col_ids = lax.broadcasted_iota(jnp.int32, (length, length), 1)
    return col_ids <= row_ids


def head_terms(query_twins, teacher_key, query_head, student_key, scale_value, mask):
    width = teacher_key.shape[-1]
    inverse = 1.0 / math.sqrt(width)
    teacher_scores = (
        jnp.einsum("hid,jd->hij", query_twins, teacher_key, preferred_element_type=jnp.float32)
        * inverse
    )
    teacher_logp = jax.nn.log_softmax(jnp.where(mask, teacher_scores, -1e30), axis=-1)
    target_logp = jnp.logaddexp(teacher_logp[0], teacher_logp[1]) - math.log(2.0)
    raw_scores = jnp.dot(query_head, student_key.T, preferred_element_type=jnp.float32) * inverse
    student_logp = jax.nn.log_softmax(jnp.where(mask, scale_value * raw_scores, -1e30), axis=-1)
    target_prob = jnp.exp(target_logp)
    student_prob = jnp.exp(student_logp)
    divergence = jnp.sum(jnp.where(mask, target_prob * (target_logp - student_logp), 0.0))
    difference = jnp.where(mask, student_prob - target_prob, 0.0)
    scale_term = jnp.sum(difference * raw_scores)
    logit_grad = (difference * (scale_value * inverse)).astype(jnp.bfloat16)
    query_grad = jnp.dot(logit_grad, student_key, preferred_element_type=jnp.float32)
    key_grad = jnp.dot(logit_grad.T, query_head, preferred_element_type=jnp.float32)
    return (query_grad, key_grad, divergence, scale_term)


def group_terms(teacher_query, teacher_key, student_query, student_key, scales, mask):
    length = teacher_key.shape[0]
    width = teacher_key.shape[1]
    heads_here = scales.shape[0]
    teacher_heads = teacher_query.reshape(length, heads_here, 2, width).transpose(1, 2, 0, 3)
    student_heads = student_query.reshape(length, heads_here, width).transpose(1, 0, 2)

    def one_head(items):
        return head_terms(items[0], teacher_key, items[1], student_key, items[2], mask)

    query_grads, key_gradient_list, divergences, scale_terms = lax.map(
        one_head, (teacher_heads, student_heads, scales)
    )
    query_grads = query_grads.transpose(1, 0, 2).reshape(length, heads_here * width)
    return (query_grads, jnp.sum(key_gradient_list, 0), jnp.sum(divergences), scale_terms)


def local_terms(teacher_query, teacher_key, student_query, student_key, scales):
    length = teacher_key.shape[0]
    groups = teacher_key.shape[1] // HEAD_WIDTH
    mask = causal_mask(length)

    def split_groups(array):
        return array.reshape(length, groups, -1).transpose(1, 0, 2)

    def group_call(items):
        return group_terms(items[0], items[1], items[2], items[3], items[4], mask)

    query_grads, key_gradient_list, divergences, scale_terms = lax.map(
        group_call,
        (
            split_groups(teacher_query),
            split_groups(teacher_key),
            split_groups(student_query),
            split_groups(student_key),
            scales.reshape(groups, -1),
        ),
    )
    query_grads = query_grads.transpose(1, 0, 2).reshape(length, -1)
    key_gradient_list = key_gradient_list.transpose(1, 0, 2).reshape(length, -1)
    return (query_grads, key_gradient_list, jnp.sum(divergences), scale_terms.reshape(-1))


def local(teacher_q, teacher_k, student_q, student_k, student_scale, pairing, placement):
    sections = lax.axis_size("section")
    section_index = lax.axis_index("section")
    slot_count = student_q.shape[1]
    layer_count = pairing.shape[0]
    layer_ids = jnp.arange(layer_count, dtype=jnp.int32)
    held_here = placement == section_index
    rank_here = jnp.cumsum(held_here.astype(jnp.int32)) - 1
    slot_ids = jnp.arange(slot_count, dtype=jnp.int32)
    slot_table = held_here[None, :] & (rank_here[None, :] == slot_ids[:, None])
    table_float = slot_table.astype(jnp.float32)
    target_layer = jnp.sum(jnp.where(pairing == section_index, layer_ids, 0))
    source_section = jnp.sum(jnp.where(layer_ids == target_layer, placement, 0))
    section_ids = jnp.arange(sections, dtype=jnp.int32)
    pair_table = (pairing[None, :] == section_ids[:, None]).astype(jnp.float32)
    route = jnp.dot(pair_table, table_float.T, precision=lax.Precision.HIGHEST).astype(jnp.bfloat16)
    outgoing_query = jnp.einsum(
        "dj,jtc->dtc", route, student_q[0], preferred_element_type=jnp.float32
    ).astype(jnp.bfloat16)
    outgoing_key = jnp.einsum(
        "dj,jtc->dtc", route, student_k[0], preferred_element_type=jnp.float32
    ).astype(jnp.bfloat16)
    arrived_query, arrived_key = (
        lax.all_to_all(outgoing_query, "section", split_axis=0, concat_axis=0, tiled=True),
        lax.all_to_all(outgoing_key, "section", split_axis=0, concat_axis=0, tiled=True),
    )
    query_layer = lax.dynamic_index_in_dim(arrived_query, source_section, 0, keepdims=False)
    key_layer = lax.dynamic_index_in_dim(arrived_key, source_section, 0, keepdims=False)
    scale_layer = lax.dynamic_index_in_dim(student_scale, target_layer, 0, keepdims=False)
    query_grad, key_grad, divergence, scale_term = local_terms(
        teacher_q[0], teacher_k[0], query_layer, key_layer, scale_layer
    )
    at_source = (section_ids == source_section)[:, None, None]
    zero_value = jnp.zeros((), jnp.bfloat16)
    back_query = jnp.where(at_source, query_grad.astype(jnp.bfloat16)[None], zero_value)
    back_key = jnp.where(at_source, key_grad.astype(jnp.bfloat16)[None], zero_value)
    returned_query, returned_key = (
        lax.all_to_all(back_query, "section", split_axis=0, concat_axis=0, tiled=True),
        lax.all_to_all(back_key, "section", split_axis=0, concat_axis=0, tiled=True),
    )
    query_grad_out = jnp.einsum(
        "dj,dtc->jtc", route, returned_query, preferred_element_type=jnp.float32
    ).astype(jnp.bfloat16)[None]
    key_grad_out = jnp.einsum(
        "dj,dtc->jtc", route, returned_key, preferred_element_type=jnp.float32
    ).astype(jnp.bfloat16)[None]
    is_target = layer_ids == target_layer
    layer_divergence = jnp.where(is_target, divergence, 0.0)
    layer_scale_terms = jnp.where(is_target[:, None], scale_term[None, :], 0.0)
    summed_divergence = lax.psum(layer_divergence, ("section", "head"))
    layer_kl_out = (summed_divergence / (STUDENT_HEADS * REPLICA_TOKENS))[None, :]
    scale_grad_out = lax.psum(layer_scale_terms, ("section", "dp"))
    return (query_grad_out, key_grad_out, layer_kl_out, scale_grad_out)


def solution(mesh):
    return jax.shard_map(
        local,
        mesh=mesh,
        in_specs=(
            P("section", "dp", "head"),
            P("section", "dp", "head"),
            P("section", None, "dp", "head"),
            P("section", None, "dp", "head"),
            P(None, "head"),
            P(),
            P(),
        ),
        out_specs=(
            P("section", None, "dp", "head"),
            P("section", None, "dp", "head"),
            P("dp", None),
            P(None, "head"),
        ),
        check_vma=False,
    )
```

profile of v0, /device:TPU:0, one launch (start us, length us, event | category | flops | bytes accessed | tf_op | source)
XLA Modules:
  0.0 140.0 jit_solution(11259147358476521377)
XLA Ops:
  2.3 1.3 convolution_convert_fusion.2
  4.3 4.2 %all-to-all-start.1 = ((bf16[4,128,256]{2,1,0:T(8,128)(2,1)}), bf16[4,128,256]{2,1,0:T(8,128)(2,1)S(1)}, u32[]{:S(2)}, u32[]{:S(2)}) async-start(bf16[4,128,256]{2,1,0:T(8,128)(2,1)} %copy.42), calls=%async_computation.1 | async-start | bytes 524288 | tf_op jit(solution)/shard_map/all_to_all | solution.py:108
  8.6 1.0 convolution_convert_fusion
  9.6 1.3 copy.38
  10.9 3.6 %all-to-all-done.1 = bf16[4,128,256]{2,1,0:T(8,128)(2,1)S(1)} async-done(((bf16[4,128,256]{2,1,0:T(8,128)(2,1)}), bf16[4,128,256]{2,1,0:T(8,128)(2,1)S(1)}, u32[]{:S(2)}, u32[]{:S(2)}) %all-to-all-start.1) | async-done | bytes 262176 | tf_op jit(solution)/shard_map/all_to_all | solution.py:108
  14.6 3.5 %all-to-all-start = ((bf16[4,128,1024]{2,1,0:T(8,128)(2,1)}), bf16[4,128,1024]{2,1,0:T(8,128)(2,1)S(1)}, u32[]{:S(2)}, u32[]{:S(2)}) async-start(bf16[4,128,1024]{2,1,0:T(8,128)(2,1)} %copy.38), calls=%async_computation | async-start | bytes 2097152 | tf_op jit(solution)/shard_map/all_to_all | solution.py:107
  18.7 1.3 select_reduce_fusion
  25.9 6.5 %all-to-all-done = bf16[4,128,1024]{2,1,0:T(8,128)(2,1)S(1)} async-done(((bf16[4,128,1024]{2,1,0:T(8,128)(2,1)}), bf16[4,128,1024]{2,1,0:T(8,128)(2,1)S(1)}, u32[]{:S(2)}, u32[]{:S(2)}) %all-to-all-start) | async-done | bytes 1048608 | tf_op jit(solution)/shard_map/all_to_all | solution.py:107
  32.7 38.8 %while.58 = (s32[]{:T(128)}, bf16[2,128,512]{1,2,0:T(8,128)(2,1)S(1)}, bf16[2,128,128]{1,2,0:T(8,128)(2,1)S(1)}, f32[2]{0:T(128)S(1)}, f32[2,4]{1,0:T(2,128)S(1)...) while((s32[]{:T(128)}, ...), condition=%wide.region_14.15_spmd.clone.clone, body=%wide.region_3.14_spmd.clone.clone.sunk | while | flops 21773572 | bytes 3401806 | solution.py:69
  33.1 17.3 %while.59 = (s32[]{:T(128)}, bf16[4,128,128]{2,1,0:T(8,128)(2,1)S(1)}, f32[4,128,128]{2,1,0:T(8,128)S(1)}, f32[4]{0:T(128)S(1)}, f32[4]{0:T(128)S(1)}, /*index=5...) while((s32[]{:T(128)}, ...), condition=%wide.region_11.11_spmd.clone, body=%wide.region_4.10_spmd.clone.sunk | while | flops 21708032 | bytes 1386189 | solution.py:51
  36.6 0.8 dynamic_update_slice.85
  40.9 0.8 dynamic_update_slice.85
  45.3 0.8 dynamic_update_slice.85
  49.6 0.8 dynamic_update_slice.85
  52.5 17.3 %while.59 = (s32[]{:T(128)}, bf16[4,128,128]{2,1,0:T(8,128)(2,1)S(1)}, f32[4,128,128]{2,1,0:T(8,128)S(1)}, f32[4]{0:T(128)S(1)}, f32[4]{0:T(128)S(1)}, /*index=5...) while((s32[]{:T(128)}, ...), condition=%wide.region_11.11_spmd.clone, body=%wide.region_4.10_spmd.clone.sunk | while | flops 21708032 | bytes 1386189 | solution.py:51
  72.6 3.4 %all-to-all-start.3 = ((bf16[4,128,256]{2,1,0:T(8,128)(2,1)}), bf16[4,128,256]{2,1,0:T(8,128)(2,1)S(1)}, u32[]{:S(2)}, u32[]{:S(2)}) async-start(bf16[4,128,256]{2,1,0:T(8,128)(2,1)} %broadcast_select_fusion.1), calls=%async_computation.3 | async-start | bytes 524288 | tf_op jit(solution)/shard_map/all_to_all | solution.py:122
  76.6 1.1 broadcast_select_fusion
  77.7 4.2 %all-to-all-done.3 = bf16[4,128,256]{2,1,0:T(8,128)(2,1)S(1)} async-done(((bf16[4,128,256]{2,1,0:T(8,128)(2,1)}), bf16[4,128,256]{2,1,0:T(8,128)(2,1)S(1)}, u32[]{:S(2)}, u32[]{:S(2)}) %all-to-all-start.3) | async-done | bytes 262176 | tf_op jit(solution)/shard_map/all_to_all | solution.py:122
  82.0 3.5 %all-to-all-start.2 = ((bf16[4,128,1024]{2,1,0:T(8,128)(2,1)}), bf16[4,128,1024]{2,1,0:T(8,128)(2,1)S(1)}, u32[]{:S(2)}, u32[]{:S(2)}) async-start(bf16[4,128,1024]{2,1,0:T(8,128)(2,1)} %broadcast_select_fusion), calls=%async_computation.2 | async-start | bytes 2097152 | tf_op jit(solution)/shard_map/all_to_all | solution.py:121
  85.5 1.3 broadcast_select_fusion.3
  87.5 35.1 %psum.14 = f32[4]{0:T(128)S(1)} all-reduce(f32[4]{0:T(128)S(1)} %broadcast_select_fusion.3), channel_id=1, replica_groups=mesh['section'=4,'head'=4,'dp'=2] {'section','head'}, use_global_device_ids=true, to_apply=%region_16.17 | all-reduce | flops 4 | bytes 32 | tf_op jit(solution)/shard_map/psum | solution.py:133
  122.7 13.9 %psum.15 = f32[4,8]{1,0:T(4,128)} all-reduce(f32[4,8]{1,0:T(4,128)S(1)} %broadcast_select_fusion.2), channel_id=1, replica_groups=mesh['section'=4,'head'=4,'dp'=2] {'section','dp'}, use_global_device_ids=true, to_apply=%region_17.18 | all-reduce | flops 32 | bytes 256 | tf_op jit(solution)/shard_map/psum | solution.py:135
  138.1 0.9 fusion.21
  139.0 0.9 copy.52
  (170 shorter events, 39.1 us)
Async XLA Ops:
  0.6 7.9 %copy-start = (bf16[1,2,128,1024]{3,2,1,0:T(8,128)(2,1)S(1)}, bf16[1,2,128,1024]{3,2,1,0:T(8,128)(2,1)}, u32[]{:S(2)}) copy-start(bf16[1,2,128,1024]{3,2,1,0:T(8,128)(2,1)} %param.13) | copy-start | bytes 1572868
  4.3 10.2 %all-to-all-start.1 = ((bf16[4,128,256]{2,1,0:T(8,128)(2,1)}), bf16[4,128,256]{2,1,0:T(8,128)(2,1)S(1)}, u32[]{:S(2)}, u32[]{:S(2)}) async-start(bf16[4,128,256]{2,1,0:T(8,128)(2,1)} %copy.42), calls=%async_computation.1 | async-start | bytes 524288 | tf_op jit(solution)/shard_map/all_to_all | solution.py:108
  10.9 7.2 %copy-start.4 = (s32[4]{0:T(128)S(1)}, s32[4]{0:T(128)}, u32[]{:S(2)}) copy-start(s32[4]{0:T(128)} %param.16) | copy-start | bytes 52
  10.9 7.8 %copy-start.3 = (s32[4]{0:T(128)S(1)}, s32[4]{0:T(128)}, u32[]{:S(2)}) copy-start(s32[4]{0:T(128)} %param.17) | copy-start | bytes 52
  10.9 13.2 %copy-start.1 = (bf16[1,128,2048]{2,1,0:T(8,128)(2,1)S(1)}, bf16[1,128,2048]{2,1,0:T(8,128)(2,1)}, u32[]{:S(2)}) copy-start(bf16[1,128,2048]{2,1,0:T(8,128)(2,1)} %param.11) | copy-start | bytes 1572868
  14.6 17.9 %all-to-all-start = ((bf16[4,128,1024]{2,1,0:T(8,128)(2,1)}), bf16[4,128,1024]{2,1,0:T(8,128)(2,1)S(1)}, u32[]{:S(2)}, u32[]{:S(2)}) async-start(bf16[4,128,1024]{2,1,0:T(8,128)(2,1)} %copy.38), calls=%async_computation | async-start | bytes 2097152 | tf_op jit(solution)/shard_map/all_to_all | solution.py:107
  18.1 6.3 %copy-start.2 = (bf16[1,128,256]{2,1,0:T(8,128)(2,1)S(1)}, bf16[1,128,256]{2,1,0:T(8,128)(2,1)}, u32[]{:S(2)}) copy-start(bf16[1,128,256]{2,1,0:T(8,128)(2,1)} %param.12) | copy-start | bytes 196612
  72.6 9.4 %all-to-all-start.3 = ((bf16[4,128,256]{2,1,0:T(8,128)(2,1)}), bf16[4,128,256]{2,1,0:T(8,128)(2,1)S(1)}, u32[]{:S(2)}, u32[]{:S(2)}) async-start(bf16[4,128,256]{2,1,0:T(8,128)(2,1)} %broadcast_select_fusion.1), calls=%async_computation.3 | async-start | bytes 524288 | tf_op jit(solution)/shard_map/all_to_all | solution.py:122
  82.0 56.2 %all-to-all-start.2 = ((bf16[4,128,1024]{2,1,0:T(8,128)(2,1)}), bf16[4,128,1024]{2,1,0:T(8,128)(2,1)S(1)}, u32[]{:S(2)}, u32[]{:S(2)}) async-start(bf16[4,128,1024]{2,1,0:T(8,128)(2,1)} %broadcast_select_fusion), calls=%async_computation.2 | async-start | bytes 2097152 | tf_op jit(solution)/shard_map/all_to_all | solution.py:121
where the time goes:
time: 141 us; the launch traced here: 140 us
  blocking collectives  49 us (35%)
  local copies, waits for them, and re-layouts  24.8 us (18%)
  other arithmetic  16.9 us (12%)
  starting transfers between devices  14.7 us (10%)
  waiting for transfers between devices  14.4 us (10%)
  matrix products  9.76 us (7%)
  loops' own time  5.65 us (4%)
  between operations  4.74 us (3%)
    psum x1, blocking collectives, local(): summed_divergence = lax.psum(layer_divergence, ('section', 'head'))  35.1 us
    psum x1, blocking collectives, local(): scale_grad_out = lax.psum(layer_scale_terms, ('section', 'dp'))  13.9 us
    dynamic_update_slice x16, local copies, waits for them, and re-layouts, group_terms(): lax.map(one_head, (teacher_heads, student_heads, scales))  11.8 us
    all_to_all x1, waiting for transfers between devices, local(): lax.all_to_all(outgoing_query, 'section', split_axis=0, concat_axis=0, ti...  6.53 us
    reduce_sum x8, other arithmetic, head_terms(): scale_term = jnp.sum(difference * raw_scores)  6.25 us
    another operation x2, loops' own time, group_terms(): lax.map(one_head, (teacher_heads, student_heads, scales))  5.41 us
    dynamic_slice x8, local copies, waits for them, and re-layouts, group_terms(): lax.map(one_head, (teacher_heads, student_heads, scales))  4.71 us
    all_to_all x1, waiting for transfers between devices, local(): lax.all_to_all(back_key, 'section', split_axis=0, concat_axis=0, tiled=True)  4.24 us
  transfers between devices with their start and end apart: 4, of which 3 were waited for; matrix products, arithmetic and copies ran while one was open for 8% of the time, Pallas kernels for 0%

commit v1 on v0

v1 whole, which is shorter than its diff:
```python
import functools
import math

import jax
import jax.numpy as jnp
from jax import lax
from jax.experimental import pallas as pl
from jax.experimental.pallas import tpu as pltpu
from jax.sharding import PartitionSpec as P

WIDTH = 128
NEG = -1e30
TINY = 1.2e-38


def kernel(
    dims,
    pairing,
    placement,
    scale,
    tq_hbm,
    tk_hbm,
    sq_hbm,
    sk_hbm,
    qg_hbm,
    kg_hbm,
    kl_ref,
    sg_ref,
    tq,
    tk,
    sq,
    sk,
    qg,
    kg,
    p_s,
    lp_s,
    g_s,
    rows_s,
    red1,
    red_dp,
    red_head,
    in_sem,
    out_sem,
    x_send,
    x_recv,
    s_send,
    s_recv,
    r1_send,
    r1_recv,
    rd_send,
    rd_recv,
    rh_send,
    rh_recv,
    *gathered,
):
    n, n_head, n_dp, tokens, heads, groups, slots, layers = dims
    chunks = heads // 2
    per_group = heads // groups
    inverse = 1.0 / math.sqrt(WIDTH)
    me = lax.axis_index("section")
    my_head = lax.axis_index("head")
    my_dp = lax.axis_index("dp")
    half = n // 2
    sibling = me + 1 - 2 * lax.rem(me, 2)

    def lanes(index):
        return slice(index * WIDTH, (index + 1) * WIDTH)

    loads_t = [pltpu.make_async_copy(tk_hbm.at[0], tk, in_sem.at[0])]
    for c in range(chunks):
        part = slice(c * 4 * WIDTH, (c + 1) * 4 * WIDTH)
        loads_t.append(
            pltpu.make_async_copy(tq_hbm.at[0, :, part], tq.at[:, part], in_sem.at[3 + c])
        )
    loads_s = [
        pltpu.make_async_copy(sk_hbm.at[0], sk, in_sem.at[1]),
        pltpu.make_async_copy(sq_hbm.at[0], sq, in_sem.at[2]),
    ]
    for copy in loads_t + loads_s:
        copy.start()

    barrier = pltpu.get_barrier_semaphore()
    peers = 0
    for axis, mine, size in (("section", me, n), ("head", my_head, n_head), ("dp", my_dp, n_dp)):
        for k in range(1, size):
            pl.semaphore_signal(
                barrier,
                inc=1,
                device_id={axis: lax.rem(mine + k, size)},
                device_id_type=pl.DeviceIdType.MESH,
            )
            peers += 1

    def remote(src, dst, send, recv, axis, peer):
        return pltpu.make_async_remote_copy(
            src_ref=src,
            dst_ref=dst,
            send_sem=send,
            recv_sem=recv,
            device_id={axis: peer},
            device_id_type=pl.DeviceIdType.MESH,
        )

    key_ids = lax.broadcasted_iota(jnp.int32, (tokens, tokens), 0)
    query_ids = lax.broadcasted_iota(jnp.int32, (tokens, tokens), 1)
    visible = key_ids <= query_ids
    strict = key_ids < query_ids
    eye = key_ids == query_ids

    count = jnp.int32(0)
    slot_layer = [jnp.int32(0)] * slots
    slot_teacher = [jnp.int32(0)] * slots
    taught = jnp.int32(0)
    for l in range(layers):
        held = placement[l] == me
        for j in range(slots):
            here = held & (count == j)
            slot_layer[j] = jnp.where(here, l, slot_layer[j])
            slot_teacher[j] = jnp.where(here, pairing[l], slot_teacher[j])
        count = count + held.astype(jnp.int32)
        taught = jnp.where(pairing[l] == me, l, taught)
    slot_valid = [count > j for j in range(slots)]

    def nt(a, b):
        return lax.dot_general(a, b, (((1,), (1,)), ((), ())), preferred_element_type=jnp.float32)

    def target(key, b):
        total = None
        for a in (2 * b, 2 * b + 1):
            s = jnp.where(visible, nt(key, tq[:, lanes(a)]) * inverse, NEG)
            e = jnp.exp(s - jnp.max(s, axis=0, keepdims=True))
            p = e * (0.5 / jnp.sum(e, axis=0, keepdims=True))
            total = p if total is None else total + p
        return total

    entropy = jnp.zeros((1, tokens), jnp.float32)
    x_copies, s_copies = [], []
    loads_t[0].wait()
    for c in range(chunks):
        loads_t[1 + c].wait()
        buffer = gathered[c]
        b = 2 * c
        first = target(tk[:, lanes(b // per_group)], b)
        second = target(tk[:, lanes((b + 1) // per_group)], b + 1)
        buffer[me, :tokens, :] = jnp.where(visible, first, second.T)
        diagonal = jnp.sum(jnp.where(eye, second, 0.0), axis=0, keepdims=True)
        buffer[me, tokens:, :] = jnp.broadcast_to(diagonal, (8, tokens))
        for t in (first, second):
            entropy = entropy + jnp.sum(t * jnp.log(jnp.maximum(t, TINY)), axis=0, keepdims=True)
        if c == 0:
            pl.semaphore_wait(barrier, peers)
        mine = buffer.at[me]
        for k in range(1, half):
            copy = remote(
                mine, mine, x_send.at[c, k], x_recv.at[c, k], "section", lax.rem(me + 2 * k, n)
            )
            copy.start()
            x_copies.append(copy)
        copy = remote(mine, mine, s_send.at[c, 0], s_recv.at[c, 0], "section", sibling)
        copy.start()
        s_copies.append(copy)

    def student(j, b):
        value = scale[slot_layer[j], b]
        raw = nt(sk[j, :, lanes(b // per_group)], sq[j, :, lanes(b)])
        z = jnp.where(visible, raw * (value * inverse), NEG)
        z = z - jnp.max(z, axis=0, keepdims=True)
        e = jnp.exp(z)
        l = jnp.sum(e, axis=0, keepdims=True)
        logp = z - jnp.log(l)
        p = e * (1.0 / l)
        p_s[j, b] = p
        lp_s[j, b] = logp
        rows_s[j * heads + b] = jnp.sum(p * logp, axis=0, keepdims=True)

    for copy in loads_s:
        copy.wait()
    for c in range(chunks):
        for j in range(slots):
            for b in (2 * c, 2 * c + 1):
                student(j, b)
        for k in range(1, half):
            x_copies[c * (half - 1) + k - 1].wait_recv()
            block = gathered[c].at[lax.rem(me + n - 2 * k, n)]
            copy = remote(block, block, s_send.at[c, k], s_recv.at[c, k], "section", sibling)
            copy.start()
            s_copies.append(copy)

    cross = [jnp.zeros((1, tokens), jnp.float32)] * slots
    scale_rows = [[None] * heads for _ in range(slots)]
    for c in range(chunks):
        for k in range(half):
            index = c if k == 0 else chunks + c * (half - 1) + k - 1
            s_copies[index].wait_recv()
        for j in range(slots):
            packed = gathered[c][slot_teacher[j], :tokens, :]
            diagonal = gathered[c][slot_teacher[j], tokens : tokens + 1, :]
            for b in (2 * c, 2 * c + 1):
                if b == 2 * c:
                    t = jnp.where(visible, packed, 0.0)
                else:
                    t = jnp.where(strict, packed.T, jnp.where(eye, diagonal, 0.0))
                value = scale[slot_layer[j], b]
                row = jnp.sum(t * lp_s[j, b], axis=0, keepdims=True)
                cross[j] = cross[j] + row
                scale_rows[j][b] = (rows_s[j * heads + b] - row) / value
                factor = jnp.where(slot_valid[j], value * inverse, 0.0)
                g_s[j, b] = ((p_s[j, b] - t) * factor).astype(jnp.bfloat16)

    tile_rows = red1.shape[1]
    row_ids = lax.broadcasted_iota(jnp.int32, (tile_rows, WIDTH), 0)
    lane_ids = lax.broadcasted_iota(jnp.int32, (tile_rows, WIDTH), 1)
    tile = jnp.where(
        (row_ids == taught) & (lane_ids == heads), jnp.sum(entropy, axis=1, keepdims=True), 0.0
    )
    for j in range(slots):
        line = jnp.where(lane_ids == heads, -jnp.sum(cross[j], axis=1, keepdims=True), 0.0)
        for b in range(heads):
            line = jnp.where(
                lane_ids == b, jnp.sum(scale_rows[j][b], axis=1, keepdims=True), line
            )
        owner = jnp.where(slot_valid[j], slot_layer[j], -1)
        tile = tile + jnp.where(row_ids == owner, line, 0.0)
    red1[me] = tile
    r1_copies = []
    for k in range(1, n):
        mine = red1.at[me]
        copy = remote(mine, mine, r1_send.at[k], r1_recv.at[k], "section", lax.rem(me + k, n))
        copy.start()
        r1_copies.append(copy)

    def gradients(j, g):
        key = sk[j, :, lanes(g)]
        total = None
        for b in range(g * per_group, (g + 1) * per_group):
            grad = g_s[j, b]
            qg[j, :, lanes(b)] = lax.dot_general(
                grad, key, (((0,), (0,)), ((), ())), preferred_element_type=jnp.float32
            ).astype(jnp.bfloat16)
            term = jnp.dot(grad, sq[j, :, lanes(b)], preferred_element_type=jnp.float32)
            total = term if total is None else total + term
        kg[j, :, lanes(g)] = total.astype(jnp.bfloat16)
        part = slice(g * per_group * WIDTH, (g + 1) * per_group * WIDTH)
        copies = [
            pltpu.make_async_copy(
                qg.at[j, :, part], qg_hbm.at[0, j, :, part], out_sem.at[0, j, g]
            ),
            pltpu.make_async_copy(
                kg.at[j, :, lanes(g)], kg_hbm.at[0, j, :, lanes(g)], out_sem.at[1, j, g]
            ),
        ]
        for copy in copies:
            copy.start()
        return copies

    units = [(j, g) for j in range(slots) for g in range(groups)]
    out_copies = []
    for unit in units[: len(units) // 2]:
        out_copies += gradients(*unit)

    for copy in r1_copies:
        copy.wait_recv()
    tile = red1[0]
    for s in range(1, n):
        tile = tile + red1[s]
    red_dp[my_dp] = tile
    red_head[my_head] = tile
    r2_copies = []
    for axis, mine, size, buffer, send, recv in (
        ("head", my_head, n_head, red_head, rh_send, rh_recv),
        ("dp", my_dp, n_dp, red_dp, rd_send, rd_recv),
    ):
        for k in range(1, size):
            block = buffer.at[mine]
            copy = remote(block, block, send.at[k], recv.at[k], axis, lax.rem(mine + k, size))
            copy.start()
            r2_copies.append(copy)

    for unit in units[len(units) // 2 :]:
        out_copies += gradients(*unit)

    for copy in r2_copies:
        copy.wait_recv()
    tile = red_dp[0]
    for s in range(1, n_dp):
        tile = tile + red_dp[s]
    sg_ref[...] = tile[:layers, :heads]
    tile = red_head[0]
    for s in range(1, n_head):
        tile = tile + red_head[s]
    column = jnp.sum(jnp.where(lane_ids == heads, tile, 0.0), axis=1, keepdims=True)
    line = jnp.sum(jnp.where(row_ids == lane_ids, column, 0.0), axis=0, keepdims=True)
    kl_ref[...] = (line / (heads * n_head * tokens))[:, :layers]

    for copy in x_copies + s_copies + r1_copies + r2_copies:
        copy.wait_send()
    for copy in out_copies:
        copy.wait()


def local(n, n_head, n_dp, teacher_q, teacher_k, student_q, student_k, student_scale, pairing, placement):
    layers, heads = student_scale.shape
    slots, tokens = student_q.shape[1:3]
    groups = student_k.shape[3] // WIDTH
    chunks = heads // 2
    tile_rows = -(-layers // 8) * 8
    dims = (n, n_head, n_dp, tokens, heads, groups, slots, layers)
    smem = pl.BlockSpec(memory_space=pltpu.SMEM)
    hbm = pl.BlockSpec(memory_space=pl.ANY)
    vmem = pl.BlockSpec(memory_space=pltpu.VMEM)
    dma = pltpu.SemaphoreType.DMA
    f32, bf16 = jnp.float32, jnp.bfloat16
    return pl.pallas_call(
        functools.partial(kernel, dims),
        out_shape=(
            jax.ShapeDtypeStruct(student_q.shape, bf16),
            jax.ShapeDtypeStruct(student_k.shape, bf16),
            jax.ShapeDtypeStruct((1, layers), f32),
            jax.ShapeDtypeStruct((layers, heads), f32),
        ),
        in_specs=[smem, smem, smem, hbm, hbm, hbm, hbm],
        out_specs=(hbm, hbm, vmem, vmem),
        scratch_shapes=[
            pltpu.VMEM(teacher_q.shape[1:], bf16),
            pltpu.VMEM(teacher_k.shape[1:], bf16),
            pltpu.VMEM(student_q.shape[1:], bf16),
            pltpu.VMEM(student_k.shape[1:], bf16),
            pltpu.VMEM(student_q.shape[1:], bf16),
            pltpu.VMEM(student_k.shape[1:], bf16),
            pltpu.VMEM((slots, heads, tokens, tokens), f32),
            pltpu.VMEM((slots, heads, tokens, tokens), f32),
            pltpu.VMEM((slots, heads, tokens, tokens), bf16),
            pltpu.VMEM((slots * heads, 1, tokens), f32),
            pltpu.VMEM((n, tile_rows, WIDTH), f32),
            pltpu.VMEM((n_dp, tile_rows, WIDTH), f32),
            pltpu.VMEM((n_head, tile_rows, WIDTH), f32),
            dma((3 + chunks,)),
            dma((2, slots, groups)),
            dma((chunks, n // 2)),
            dma((chunks, n // 2)),
            dma((chunks, n // 2)),
            dma((chunks, n // 2)),
            dma((n,)),
            dma((n,)),
            dma((n_dp,)),
            dma((n_dp,)),
            dma((n_head,)),
            dma((n_head,)),
        ]
        + [pltpu.VMEM((n, tokens + 8, tokens), f32) for _ in range(chunks)],
        compiler_params=pltpu.CompilerParams(collective_id=0, has_side_effects=True),
    )(pairing, placement, student_scale, teacher_q, teacher_k, student_q, student_k)


def solution(mesh):
    sizes = (mesh.shape["section"], mesh.shape["head"], mesh.shape["dp"])
    return jax.shard_map(
        functools.partial(local, *sizes),
        mesh=mesh,
        in_specs=(
            P("section", "dp", "head"),
            P("section", "dp", "head"),
            P("section", None, "dp", "head"),
            P("section", None, "dp", "head"),
            P(None, "head"),
            P(),
            P(),
        ),
        out_specs=(
            P("section", None, "dp", "head"),
            P("section", None, "dp", "head"),
            P("dp", None),
            P(None, "head"),
        ),
        check_vma=False,
    )
```

time: 141 us -> 26.1 us (0.19)
  blocking collectives: 49 us -> 0 us
  Pallas kernels: 0 us -> 21.5 us
  local copies, waits for them, and re-layouts: 24.8 us -> 3.66 us
  other arithmetic: 16.9 us -> 0 us
  starting transfers between devices: 14.7 us -> 0 us
  waiting for transfers between devices: 14.4 us -> 0 us
  matrix products: 9.76 us -> 0 us
  loops' own time: 5.65 us -> 0 us
  between operations: 4.74 us -> 0.65 us
    psum x2 -> x0, blocking collectives: 49 us -> none  [the longest x1 35.1 us: local(): summed_divergence = lax.psum(layer_divergence, ('section', 'head'))]
    pallas_call x0 -> x1, Pallas kernels: none -> 21.5 us  [local(): pl.pallas_call(functools.partial(kernel, dims), out_shape=(jax.ShapeDtype...]
    all_to_all x4 -> x0, starting transfers between devices: 14.7 us -> none  [the longest x1 4.23 us: local(): lax.all_to_all(outgoing_key, 'section', split_axis=0, concat_axis=0, tile...]
    all_to_all x4 -> x0, waiting for transfers between devices: 14.4 us -> none  [the longest x1 6.53 us: local(): lax.all_to_all(outgoing_query, 'section', split_axis=0, concat_axis=0, ti...]
    dynamic_update_slice x28 -> x0, local copies, waits for them, and re-layouts: 13.9 us -> none  [the longest x16 11.8 us: group_terms(): lax.map(one_head, (teacher_heads, student_heads, scales))]
    reduce_sum x31 -> x0, other arithmetic: 10.7 us -> none  [the longest x8 6.25 us: head_terms(): scale_term = jnp.sum(difference * raw_scores)]
    dot_general x37 -> x0, matrix products: 9.76 us -> none  [the longest x8 1.72 us: head_terms(): jnp.dot(logit_grad, student_key, preferred_element_type=jnp.float32)]
    dynamic_slice x21 -> x0, local copies, waits for them, and re-layouts: 6.02 us -> none  [the longest x8 4.71 us: group_terms(): lax.map(one_head, (teacher_heads, student_heads, scales))]
  transfers between devices with their start and end apart: 4 -> 0, of which waited for: 3 -> 0; matrix products, arithmetic and copies ran while one was open for 8% -> 0% of each run, Pallas kernels for 0% -> 0%
where the time goes in v1:
time: 26.1 us; the launch traced here: 25.9 us
  Pallas kernels  21.5 us (82%)
  local copies, waits for them, and re-layouts  3.66 us (14%)
  between operations  0.65 us (2%)
    pallas_call x1, Pallas kernels, local(): pl.pallas_call(functools.partial(kernel, dims), out_shape=(jax.ShapeDtype...  21.5 us
    unnamed x10, local copies, waits for them, and re-layouts  3.66 us

profile of v1, /device:TPU:0, one launch (start us, length us, event | category | flops | bytes accessed | tf_op | source)
XLA Modules:
  0.0 25.9 jit_solution(1041916316107187923)
XLA Ops:
  0.6 21.5 %shard_map.102 = (bf16[1,2,128,1024]{3,2,1,0:T(8,128)(2,1)}, bf16[1,2,128,256]{3,2,1,0:T(8,128)(2,1)}, f32[1,4]{1,0:T(1,128)}, f32[4,8]{1,0:T(4,128)}) custom-call(s32[4]{0:T(128)} %pairing.1, s32[4]{0:T(128)} %placement.1, f32[4,8]{1,0:T(4,128)} %scale.1, bf16[1,128,2048]{2,1,0:T(8,128)(2,1)} %tq_hbm.1, bf16[1,128,256]{2,1,0:T(8,128)(2,1)} %tk_hbm.1, ...), custom_call_target="tpu_custom_call" | custom-call | tf_op jit(solution)/shard_map/pallas_call | solution.py:313
  22.2 0.0 copy-start
  22.2 1.9 %copy.15 = bf16[1,2,128,1024]{3,2,1,0:T(8,128)(2,1)} copy(bf16[1,2,128,1024]{3,2,1,0:T(8,128)(2,1)} %get-tuple-element.8) | data formatting | bytes 1048576
  24.1 0.0 copy-done
  24.1 0.0 copy-start.2
  24.1 0.0 copy-start.1
  24.1 0.7 %copy.16 = bf16[1,2,128,256]{3,2,1,0:T(8,128)(2,1)} copy(bf16[1,2,128,256]{3,2,1,0:T(8,128)(2,1)S(1)} %copy-done) | data formatting | bytes 262144
  24.8 0.0 copy-done.2
  24.8 0.5 %copy.17 = f32[1,4]{1,0:T(1,128)} copy(f32[1,4]{1,0:T(1,128)S(1)} %copy-done.2) | data formatting | bytes 32
  25.3 0.0 copy-done.1
  25.3 0.6 %copy.18 = f32[4,8]{1,0:T(4,128)} copy(f32[4,8]{1,0:T(4,128)S(1)} %copy-done.1) | data formatting | bytes 256
Async XLA Ops:
  22.2 1.9 %copy-start = (bf16[1,2,128,256]{3,2,1,0:T(8,128)(2,1)S(1)}, bf16[1,2,128,256]{3,2,1,0:T(8,128)(2,1)}, u32[]{:S(2)}) copy-start(bf16[1,2,128,256]{3,2,1,0:T(8,128)(2,1)} %get-tuple-element.9) | copy-start | bytes 393220
  24.1 0.7 %copy-start.2 = (f32[1,4]{1,0:T(1,128)S(1)}, f32[1,4]{1,0:T(1,128)}, u32[]{:S(2)}) copy-start(f32[1,4]{1,0:T(1,128)} %get-tuple-element.10) | copy-start | bytes 52
  24.1 1.2 %copy-start.1 = (f32[4,8]{1,0:T(4,128)S(1)}, f32[4,8]{1,0:T(4,128)}, u32[]{:S(2)}) copy-start(f32[4,8]{1,0:T(4,128)} %get-tuple-element.11) | copy-start | bytes 388

commit v2 on v1

v2 whole, which is shorter than its diff:
```python
import functools
import math

import jax
import jax.numpy as jnp
from jax import lax
from jax.experimental import pallas as pl
from jax.experimental.pallas import tpu as pltpu
from jax.sharding import PartitionSpec as P

WIDTH = 128
NEG = -1e30
TINY = 1.2e-38


def kernel(
    dims,
    pairing,
    placement,
    scale,
    tq_hbm,
    tk_hbm,
    sq_hbm,
    sk_hbm,
    qg,
    kg,
    kl_ref,
    sg_ref,
    tq,
    tk,
    sq,
    sk,
    p_s,
    lp_s,
    g_s,
    rows_s,
    red_dp,
    red_head,
    in_sem,
    x_send,
    x_recv,
    s_send,
    s_recv,
    rd_send,
    rd_recv,
    rh_send,
    rh_recv,
    *gathered,
):
    n, n_head, n_dp, tokens, heads, groups, slots, layers = dims
    chunks = heads // 2
    per_group = heads // groups
    inverse = 1.0 / math.sqrt(WIDTH)
    me = lax.axis_index("section")
    my_head = lax.axis_index("head")
    my_dp = lax.axis_index("dp")
    half = n // 2
    sibling = me + 1 - 2 * lax.rem(me, 2)

    def lanes(index):
        return slice(index * WIDTH, (index + 1) * WIDTH)

    loads_t = [pltpu.make_async_copy(tk_hbm.at[0], tk, in_sem.at[0])]
    for c in range(chunks):
        part = slice(c * 4 * WIDTH, (c + 1) * 4 * WIDTH)
        loads_t.append(
            pltpu.make_async_copy(tq_hbm.at[0, :, part], tq.at[:, part], in_sem.at[3 + c])
        )
    loads_s = [
        pltpu.make_async_copy(sk_hbm.at[0], sk, in_sem.at[1]),
        pltpu.make_async_copy(sq_hbm.at[0], sq, in_sem.at[2]),
    ]
    for copy in loads_t + loads_s:
        copy.start()

    barrier = pltpu.get_barrier_semaphore()
    dp_peers = [
        ({"section": lax.rem(me + k, n), "dp": lax.rem(my_dp + d, n_dp)}, (k, d))
        for d in range(n_dp)
        for k in range(n)
        if (k, d) != (0, 0)
    ]
    head_peers = [
        ({"section": lax.rem(me + k, n), "head": lax.rem(my_head + h, n_head)}, (k, h))
        for h in range(1, n_head)
        for k in range(n)
    ]
    for peer, _ in dp_peers + head_peers:
        pl.semaphore_signal(barrier, inc=1, device_id=peer, device_id_type=pl.DeviceIdType.MESH)
    peers = len(dp_peers) + len(head_peers)

    def send(src, dst, send_sem, recv_sem, peer):
        return pltpu.make_async_remote_copy(
            src_ref=src,
            dst_ref=dst,
            send_sem=send_sem,
            recv_sem=recv_sem,
            device_id=peer,
            device_id_type=pl.DeviceIdType.MESH,
        )

    def remote(src, dst, send_sem, recv_sem, peer):
        return send(src, dst, send_sem, recv_sem, {"section": peer})

    key_ids = lax.broadcasted_iota(jnp.int32, (tokens, tokens), 0)
    query_ids = lax.broadcasted_iota(jnp.int32, (tokens, tokens), 1)
    visible = key_ids <= query_ids
    strict = key_ids < query_ids
    eye = key_ids == query_ids

    count = jnp.int32(0)
    slot_layer = [jnp.int32(0)] * slots
    slot_teacher = [jnp.int32(0)] * slots
    taught = jnp.int32(0)
    for l in range(layers):
        held = placement[l] == me
        for j in range(slots):
            here = held & (count == j)
            slot_layer[j] = jnp.where(here, l, slot_layer[j])
            slot_teacher[j] = jnp.where(here, pairing[l], slot_teacher[j])
        count = count + held.astype(jnp.int32)
        taught = jnp.where(pairing[l] == me, l, taught)
    slot_valid = [count > j for j in range(slots)]

    def nt(a, b):
        return lax.dot_general(a, b, (((1,), (1,)), ((), ())), preferred_element_type=jnp.float32)

    def target(key, b):
        total = None
        for a in (2 * b, 2 * b + 1):
            s = jnp.where(visible, nt(key, tq[:, lanes(a)]) * inverse, NEG)
            e = jnp.exp(s - jnp.max(s, axis=0, keepdims=True))
            p = e * (0.5 / jnp.sum(e, axis=0, keepdims=True))
            total = p if total is None else total + p
        return total

    entropy = jnp.zeros((1, tokens), jnp.float32)
    x_copies, s_copies = [], []
    loads_t[0].wait()
    for c in range(chunks):
        loads_t[1 + c].wait()
        buffer = gathered[c]
        b = 2 * c
        first = target(tk[:, lanes(b // per_group)], b)
        second = target(tk[:, lanes((b + 1) // per_group)], b + 1)
        buffer[me, :tokens, :] = jnp.where(visible, first, second.T)
        diagonal = jnp.sum(jnp.where(eye, second, 0.0), axis=0, keepdims=True)
        buffer[me, tokens:, :] = jnp.broadcast_to(diagonal, (8, tokens))
        for t in (first, second):
            entropy = entropy + jnp.sum(t * jnp.log(jnp.maximum(t, TINY)), axis=0, keepdims=True)
        if c == 0:
            pl.semaphore_wait(barrier, peers)
        mine = buffer.at[me]
        for k in range(1, half):
            copy = remote(
                mine, mine, x_send.at[c, k], x_recv.at[c, k], lax.rem(me + 2 * k, n)
            )
            copy.start()
            x_copies.append(copy)
        copy = remote(mine, mine, s_send.at[c, 0], s_recv.at[c, 0], sibling)
        copy.start()
        s_copies.append(copy)

    def student(j, b):
        value = scale[slot_layer[j], b]
        raw = nt(sk[j, :, lanes(b // per_group)], sq[j, :, lanes(b)])
        z = jnp.where(visible, raw * (value * inverse), NEG)
        z = z - jnp.max(z, axis=0, keepdims=True)
        e = jnp.exp(z)
        l = jnp.sum(e, axis=0, keepdims=True)
        logp = z - jnp.log(l)
        p = e * (1.0 / l)
        p_s[j, b] = p
        lp_s[j, b] = logp
        rows_s[j, b : b + 1, :] = jnp.sum(p * logp, axis=0, keepdims=True)

    cross = [jnp.zeros((1, tokens), jnp.float32)] * slots

    def compare(c):
        for k in range(half):
            index = c if k == 0 else chunks + c * (half - 1) + k - 1
            s_copies[index].wait_recv()
        for j in range(slots):
            packed = gathered[c][slot_teacher[j], :tokens, :]
            diagonal = gathered[c][slot_teacher[j], tokens : tokens + 1, :]
            for b in (2 * c, 2 * c + 1):
                if b == 2 * c:
                    t = jnp.where(visible, packed, 0.0)
                else:
                    t = jnp.where(strict, packed.T, jnp.where(eye, diagonal, 0.0))
                value = scale[slot_layer[j], b]
                row = jnp.sum(t * lp_s[j, b], axis=0, keepdims=True)
                cross[j] = cross[j] + row
                spot = slice(b, b + 1)
                rows_s[j, spot, :] = (rows_s[j, spot, :] - row) / value
                factor = jnp.where(slot_valid[j], value * inverse, 0.0)
                g_s[j, b] = ((p_s[j, b] - t) * factor).astype(jnp.bfloat16)

    def gradients(j, g):
        key = sk[j, :, lanes(g)]
        total = None
        for b in range(g * per_group, (g + 1) * per_group):
            grad = g_s[j, b]
            qg[0, j, :, lanes(b)] = lax.dot_general(
                grad, key, (((0,), (0,)), ((), ())), preferred_element_type=jnp.float32
            ).astype(jnp.bfloat16)
            term = jnp.dot(grad, sq[j, :, lanes(b)], preferred_element_type=jnp.float32)
            total = term if total is None else total + term
        kg[0, j, :, lanes(g)] = total.astype(jnp.bfloat16)

    ready = 0

    def finished_groups(heads_done, first):
        last = heads_done // per_group
        for g in range(first, last):
            for j in range(slots):
                gradients(j, g)
        return last

    for copy in loads_s:
        copy.wait()
    for c in range(chunks):
        for j in range(slots):
            for b in (2 * c, 2 * c + 1):
                student(j, b)
        for k in range(1, half):
            x_copies[c * (half - 1) + k - 1].wait_recv()
            block = gathered[c].at[lax.rem(me + n - 2 * k, n)]
            copy = remote(block, block, s_send.at[c, k], s_recv.at[c, k], sibling)
            copy.start()
            s_copies.append(copy)
        if c > 0:
            ready = finished_groups(2 * (c - 1), ready)
            compare(c - 1)
    ready = finished_groups(2 * (chunks - 1), ready)
    compare(chunks - 1)

    tile_rows = red_dp.shape[2]
    row_ids = lax.broadcasted_iota(jnp.int32, (tile_rows, WIDTH), 0)
    lane_ids = lax.broadcasted_iota(jnp.int32, (tile_rows, WIDTH), 1)
    head_rows = lax.broadcasted_iota(jnp.int32, (heads, WIDTH), 0)
    head_lanes = lax.broadcasted_iota(jnp.int32, (heads, WIDTH), 1)
    tile = jnp.where(
        (row_ids == taught) & (lane_ids == heads), jnp.sum(entropy, axis=1, keepdims=True), 0.0
    )
    for j in range(slots):
        column = jnp.sum(rows_s[j], axis=1, keepdims=True)
        line = jnp.sum(jnp.where(head_rows == head_lanes, column, 0.0), axis=0, keepdims=True)
        line = jnp.where(lane_ids == heads, -jnp.sum(cross[j], axis=1, keepdims=True), line)
        owner = jnp.where(slot_valid[j], slot_layer[j], -1)
        tile = tile + jnp.where(row_ids == owner, line, 0.0)
    red_dp[me, my_dp] = tile
    mine = red_dp.at[me, my_dp]
    r_copies = []
    for peer, (k, h) in head_peers:
        r_copies.append(
            send(mine, red_head.at[me, my_head], rh_send.at[k, h], rh_recv.at[k, h], peer)
        )
    for peer, (k, d) in dp_peers:
        r_copies.append(send(mine, mine, rd_send.at[k, d], rd_recv.at[k, d], peer))
    for copy in r_copies:
        copy.start()

    finished_groups(heads, ready)

    for copy in r_copies:
        copy.wait_recv()
    for s in range(n):
        red_head[s, my_head] = red_dp[s, my_dp]

    def added(buffer, size):
        total = None
        for a in range(size):
            for s in range(n):
                total = buffer[s, a] if total is None else total + buffer[s, a]
        return total

    sg_ref[...] = added(red_dp, n_dp)[:layers, :heads]
    column = jnp.sum(
        jnp.where(lane_ids == heads, added(red_head, n_head), 0.0), axis=1, keepdims=True
    )
    line = jnp.sum(jnp.where(row_ids == lane_ids, column, 0.0), axis=0, keepdims=True)
    kl_ref[...] = (line / (heads * n_head * tokens))[:, :layers]

    for copy in x_copies + s_copies + r_copies:
        copy.wait_send()


def hand_out(*refs):
    count = len(refs) // 2
    sems = refs[-1]
    copies = [
        pltpu.make_async_copy(refs[i], refs[count + i], sems.at[i]) for i in range(count)
    ]
    for copy in copies:
        copy.start()
    for copy in copies:
        copy.wait()


def local(n, n_head, n_dp, teacher_q, teacher_k, student_q, student_k, student_scale, pairing, placement):
    layers, heads = student_scale.shape
    slots, tokens = student_q.shape[1:3]
    groups = student_k.shape[3] // WIDTH
    chunks = heads // 2
    tile_rows = -(-layers // 8) * 8
    dims = (n, n_head, n_dp, tokens, heads, groups, slots, layers)
    smem = pl.BlockSpec(memory_space=pltpu.SMEM)
    hbm = pl.BlockSpec(memory_space=pltpu.HBM)
    vmem = pl.BlockSpec(memory_space=pltpu.VMEM)
    dma = pltpu.SemaphoreType.DMA
    f32, bf16 = jnp.float32, jnp.bfloat16
    shapes = (
        (student_q.shape, bf16),
        (student_k.shape, bf16),
        ((1, layers), f32),
        ((layers, heads), f32),
    )
    results = pl.pallas_call(
        functools.partial(kernel, dims),
        out_shape=tuple(pltpu.VMEM(*shape) for shape in shapes),
        in_specs=[smem, smem, smem, hbm, hbm, hbm, hbm],
        out_specs=(vmem,) * 4,
        scratch_shapes=[
            pltpu.VMEM(teacher_q.shape[1:], bf16),
            pltpu.VMEM(teacher_k.shape[1:], bf16),
            pltpu.VMEM(student_q.shape[1:], bf16),
            pltpu.VMEM(student_k.shape[1:], bf16),
            pltpu.VMEM((slots, heads, tokens, tokens), f32),
            pltpu.VMEM((slots, heads, tokens, tokens), f32),
            pltpu.VMEM((slots, heads, tokens, tokens), bf16),
            pltpu.VMEM((slots, heads, tokens), f32),
            pltpu.VMEM((n, n_dp, tile_rows, WIDTH), f32),
            pltpu.VMEM((n, n_head, tile_rows, WIDTH), f32),
            dma((3 + chunks,)),
            dma((chunks, n // 2)),
            dma((chunks, n // 2)),
            dma((chunks, n // 2)),
            dma((chunks, n // 2)),
            dma((n, n_dp)),
            dma((n, n_dp)),
            dma((n, n_head)),
            dma((n, n_head)),
        ]
        + [pltpu.VMEM((n, tokens + 8, tokens), f32) for _ in range(chunks)],
        compiler_params=pltpu.CompilerParams(
            collective_id=0, has_side_effects=True, vmem_limit_bytes=56 * 1024 * 1024
        ),
    )(pairing, placement, student_scale, teacher_q, teacher_k, student_q, student_k)
    return pl.pallas_call(
        hand_out,
        out_shape=tuple(jax.ShapeDtypeStruct(*shape) for shape in shapes),
        in_specs=[vmem] * 4,
        out_specs=(hbm,) * 4,
        scratch_shapes=[dma((4,))],
        compiler_params=pltpu.CompilerParams(vmem_limit_bytes=4 * 1024 * 1024),
    )(*results)


def solution(mesh):
    sizes = (mesh.shape["section"], mesh.shape["head"], mesh.shape["dp"])
    return jax.shard_map(
        functools.partial(local, *sizes),
        mesh=mesh,
        in_specs=(
            P("section", "dp", "head"),
            P("section", "dp", "head"),
            P("section", None, "dp", "head"),
            P("section", None, "dp", "head"),
            P(None, "head"),
            P(),
            P(),
        ),
        out_specs=(
            P("section", None, "dp", "head"),
            P("section", None, "dp", "head"),
            P("dp", None),
            P(None, "head"),
        ),
        check_vma=False,
    )
```

time: 26.1 us -> 22.2 us (0.85)
  local copies, waits for them, and re-layouts: 3.66 us -> 0 us
    unnamed x10 -> x0, local copies, waits for them, and re-layouts: 3.66 us -> none
    pallas_call x1 -> x2, Pallas kernels: 21.5 us -> 21.4 us  [the longest x1 20.6 us: local(): pl.pallas_call(functools.partial(kernel, dims), out_shape=tuple((pltpu.VM...]
where the time goes in v2:
time: 22.2 us; the launch traced here: 22.1 us
  Pallas kernels  21.4 us (96%)
  between operations  0.64 us (3%)
    pallas_call x1, Pallas kernels, local(): pl.pallas_call(functools.partial(kernel, dims), out_shape=tuple((pltpu.VM...  20.6 us
    pallas_call x1, Pallas kernels, local(): pl.pallas_call(hand_out, out_shape=tuple((jax.ShapeDtypeStruct(*shape) fo...  0.87 us

profile of v2, /device:TPU:0, one launch (start us, length us, event | category | flops | bytes accessed | tf_op | source)
XLA Modules:
  0.0 22.1 jit_solution(10239108776093651773)
XLA Ops:
  0.6 20.6 %shard_map.102 = (bf16[1,2,128,1024]{3,2,1,0:T(8,128)(2,1)S(1)}, bf16[1,2,128,256]{3,2,1,0:T(8,128)(2,1)S(1)}, f32[1,4]{1,0:T(1,128)S(1)}, f32[4,8]{1,0:T(4,128)S(1)}) custom-call(s32[4]{0:T(128)} %pairing.1, s32[4]{0:T(128)} %placement.1, f32[4,8]{1,0:T(4,128)} %scale.1, bf16[1,128,2048]{2,1,0:T(8,128)(2,1)} %tq_hbm.1, bf16[1,128,256]{2,1,0:T(8,128)(2,1)} %tk_hbm.1, ...), custom_call_target="tpu_custom_call" | custom-call | tf_op jit(solution)/shard_map/pallas_call | solution.py:319
  21.2 0.9 %shard_map.103 = (bf16[1,2,128,1024]{3,2,1,0:T(8,128)(2,1)}, bf16[1,2,128,256]{3,2,1,0:T(8,128)(2,1)}, f32[1,4]{1,0:T(1,128)}, f32[4,8]{1,0:T(4,128)}) custom-call(bf16[1,2,128,1024]{3,2,1,0:T(8,128)(2,1)S(1)} %get-tuple-element.8.refs_0_, bf16[1,2,128,256]{3,2,1,0:T(8,128)(2,1)S(1)} %get-tuple-element.9.refs_1_, f32[1,4]{1,0:T(1,128)S(1)} %get-tuple-element.10.refs_2_, ...), custom_call_target="tpu_custom_call" | custom-call | tf_op jit(solution)/shard_map/pallas_call | solution.py:350

commit v3 on v2

--- a/solution.py
+++ b/solution.py
@@ -15,9 +15,9 @@
 
 def kernel(
     dims,
-    pairing,
-    placement,
-    scale,
+    pairing_hbm,
+    placement_hbm,
+    scale_hbm,
     tq_hbm,
     tk_hbm,
     sq_hbm,
@@ -36,6 +36,9 @@
     rows_s,
     red_dp,
     red_head,
+    pairing,
+    placement,
+    scale,
     in_sem,
     x_send,
     x_recv,
@@ -66,11 +69,16 @@
         loads_t.append(
             pltpu.make_async_copy(tq_hbm.at[0, :, part], tq.at[:, part], in_sem.at[3 + c])
         )
+    loads_small = [
+        pltpu.make_async_copy(pairing_hbm, pairing, in_sem.at[3 + chunks]),
+        pltpu.make_async_copy(placement_hbm, placement, in_sem.at[4 + chunks]),
+        pltpu.make_async_copy(scale_hbm, scale, in_sem.at[5 + chunks]),
+    ]
     loads_s = [
         pltpu.make_async_copy(sk_hbm.at[0], sk, in_sem.at[1]),
         pltpu.make_async_copy(sq_hbm.at[0], sq, in_sem.at[2]),
     ]
-    for copy in loads_t + loads_s:
+    for copy in loads_t + loads_small + loads_s:
         copy.start()
 
     barrier = pltpu.get_barrier_semaphore()
@@ -107,20 +115,6 @@
     visible = key_ids <= query_ids
     strict = key_ids < query_ids
     eye = key_ids == query_ids
-
-    count = jnp.int32(0)
-    slot_layer = [jnp.int32(0)] * slots
-    slot_teacher = [jnp.int32(0)] * slots
-    taught = jnp.int32(0)
-    for l in range(layers):
-        held = placement[l] == me
-        for j in range(slots):
-            here = held & (count == j)
-            slot_layer[j] = jnp.where(here, l, slot_layer[j])
-            slot_teacher[j] = jnp.where(here, pairing[l], slot_teacher[j])
-        count = count + held.astype(jnp.int32)
-        taught = jnp.where(pairing[l] == me, l, taught)
-    slot_valid = [count > j for j in range(slots)]
 
     def nt(a, b):
         return lax.dot_general(a, b, (((1,), (1,)), ((), ())), preferred_element_type=jnp.float32)
@@ -150,7 +144,7 @@
             entropy = entropy + jnp.sum(t * jnp.log(jnp.maximum(t, TINY)), axis=0, keepdims=True)
         if c == 0:
             pl.semaphore_wait(barrier, peers)
-        mine = buffer.at[me]
+        mine = buffer.at[me, : tokens + 1]
         for k in range(1, half):
             copy = remote(
                 mine, mine, x_send.at[c, k], x_recv.at[c, k], lax.rem(me + 2 * k, n)
@@ -160,6 +154,23 @@
         copy = remote(mine, mine, s_send.at[c, 0], s_recv.at[c, 0], sibling)
         copy.start()
         s_copies.append(copy)
+
+    for copy in loads_small:
+        copy.wait()
+
+    count = jnp.int32(0)
+    slot_layer = [jnp.int32(0)] * slots
+    slot_teacher = [jnp.int32(0)] * slots
+    taught = jnp.int32(0)
+    for l in range(layers):
+        held = placement[l] == me
+        for j in range(slots):
+            here = held & (count == j)
+            slot_layer[j] = jnp.where(here, l, slot_layer[j])
+            slot_teacher[j] = jnp.where(here, pairing[l], slot_teacher[j])
+        count = count + held.astype(jnp.int32)
+        taught = jnp.where(pairing[l] == me, l, taught)
+    slot_valid = [count > j for j in range(slots)]
 
     def student(j, b):
         value = scale[slot_layer[j], b]
@@ -225,7 +236,7 @@
                 student(j, b)
         for k in range(1, half):
             x_copies[c * (half - 1) + k - 1].wait_recv()
-            block = gathered[c].at[lax.rem(me + n - 2 * k, n)]
+            block = gathered[c].at[lax.rem(me + n - 2 * k, n), : tokens + 1]
             copy = remote(block, block, s_send.at[c, k], s_recv.at[c, k], sibling)
             copy.start()
             s_copies.append(copy)
@@ -305,7 +316,6 @@
     chunks = heads // 2
     tile_rows = -(-layers // 8) * 8
     dims = (n, n_head, n_dp, tokens, heads, groups, slots, layers)
-    smem = pl.BlockSpec(memory_space=pltpu.SMEM)
     hbm = pl.BlockSpec(memory_space=pltpu.HBM)
     vmem = pl.BlockSpec(memory_space=pltpu.VMEM)
     dma = pltpu.SemaphoreType.DMA
@@ -319,7 +329,7 @@
     results = pl.pallas_call(
         functools.partial(kernel, dims),
         out_shape=tuple(pltpu.VMEM(*shape) for shape in shapes),
-        in_specs=[smem, smem, smem, hbm, hbm, hbm, hbm],
+        in_specs=[hbm] * 7,
         out_specs=(vmem,) * 4,
         scratch_shapes=[
             pltpu.VMEM(teacher_q.shape[1:], bf16),
@@ -332,7 +342,10 @@
             pltpu.VMEM((slots, heads, tokens), f32),
             pltpu.VMEM((n, n_dp, tile_rows, WIDTH), f32),
             pltpu.VMEM((n, n_head, tile_rows, WIDTH), f32),
-            dma((3 + chunks,)),
+            pltpu.SMEM(pairing.shape, jnp.int32),
+            pltpu.SMEM(placement.shape, jnp.int32),
+            pltpu.SMEM(student_scale.shape, f32),
+            dma((6 + chunks,)),
             dma((chunks, n // 2)),
             dma((chunks, n // 2)),
             dma((chunks, n // 2)),

time: 22.2 us -> 21.3 us (0.959)
  Pallas kernels: 21.4 us -> 20.5 us
    pallas_call x1, Pallas kernels: 20.6 us -> 19.6 us  [local(): pl.pallas_call(functools.partial(kernel, dims), out_shape=tuple((pltpu.VM...]
where the time goes in v3:
time: 21.3 us; the launch traced here: 21.1 us
  Pallas kernels  20.5 us (96%)
  between operations  0.64 us (3%)
    pallas_call x1, Pallas kernels, local(): pl.pallas_call(functools.partial(kernel, dims), out_shape=tuple((pltpu.VM...  19.6 us
    pallas_call x1, Pallas kernels, local(): pl.pallas_call(hand_out, out_shape=tuple((jax.ShapeDtypeStruct(*shape) fo...  0.87 us

profile of v3, /device:TPU:0, one launch (start us, length us, event | category | flops | bytes accessed | tf_op | source)
XLA Modules:
  0.0 21.1 jit_solution(4732399608413818130)
XLA Ops:
  0.6 19.6 %shard_map.102 = (bf16[1,2,128,1024]{3,2,1,0:T(8,128)(2,1)S(1)}, bf16[1,2,128,256]{3,2,1,0:T(8,128)(2,1)S(1)}, f32[1,4]{1,0:T(1,128)S(1)}, f32[4,8]{1,0:T(4,128)S(1)}) custom-call(s32[4]{0:T(128)} %pairing_hbm.1, s32[4]{0:T(128)} %placement_hbm.1, f32[4,8]{1,0:T(4,128)} %scale_hbm.1, bf16[1,128,2048]{2,1,0:T(8,128)(2,1)} %tq_hbm.1, ...), custom_call_target="tpu_custom_call" | custom-call | tf_op jit(solution)/shard_map/pallas_call | solution.py:329
  20.2 0.9 %shard_map.103 = (bf16[1,2,128,1024]{3,2,1,0:T(8,128)(2,1)}, bf16[1,2,128,256]{3,2,1,0:T(8,128)(2,1)}, f32[1,4]{1,0:T(1,128)}, f32[4,8]{1,0:T(4,128)}) custom-call(bf16[1,2,128,1024]{3,2,1,0:T(8,128)(2,1)S(1)} %get-tuple-element.8.refs_0_, bf16[1,2,128,256]{3,2,1,0:T(8,128)(2,1)S(1)} %get-tuple-element.9.refs_1_, f32[1,4]{1,0:T(1,128)S(1)} %get-tuple-element.10.refs_2_, ...), custom_call_target="tpu_custom_call" | custom-call | tf_op jit(solution)/shard_map/pallas_call | solution.py:363
